TPU v7x, 256 devices: a whole 4x4x8 slice. The times are simulated.
256 devices in a mesh: gx: 16 (over z, core), gy: 8 (over x_hi, y), gz: 2 (over x_lo).
Axes of the slice: x: 4 (x_hi: 2, x_lo: 2; x = x_hi * 2 + x_lo), y: 4, z: 8, core: 2. Of those that a mesh axis runs over, the one named last changes fastest.
Arguments:
- load_current: float32 [1536, 8192], P('gy', 'gx'), may hold values from 0 to 90
- sink_mask: int32 [1536, 8192], P('gy', 'gx'), may hold values 0 or 1
- pad_mask: int32 [1536, 8192], P('gy', 'gx'), may hold values from 0 to 1, as said below
- plane_class: int32 [4, 1536, 8192], P('gz', 'gy', 'gx'), may hold values from 0 to 7
- via_class: int32 [4, 1536, 8192], P('gz', 'gy', 'gx'), may hold values from 0 to 7
- plane_table: float32 [4, 8], P('gz'), may hold values from 0.25 to 4
- via_table: float32 [4, 8], P('gz'), may hold values from 0.25 to 4
Outputs:
- voltage: float32 [4, 1536, 8192], P('gz', 'gy', 'gx')
- residual: float32 [4, 1536, 8192], P('gz', 'gy', 'gx')
Inputs may be any that keep to these rules, and one draw needn't show every extreme that they name: `pad_mask`: exactly one pad in each aligned 8 x 8 tile of nodes.
All inputs are finite; a program needn't handle non-finite values. No bound on the sum of `sink_mask` on one device may be relied on, other than what follows from the above.
Results may differ from a plain program's by a relative error of at most 0.00012.
Values sent between devices are 32-bit elements; how exact they have to be, the bound alone decides.
A program may use at most 64 MiB of HBM per device.

v0:
```python
import jax
import jax.numpy as jnp
from jax import lax
from jax.sharding import Mesh
from jax.sharding import PartitionSpec as P

ITERS = 3
GX = ("gx_0", "gx_1")
GY = ("gy_0", "gy_1")
GX_GY_GZ = ("gx_0", "gx_1", "gy_0", "gy_1", "gz")
PAD_CONDUCTANCE = 20.0


def padded(array, sides, width):
    edges = {}
    for axis, dim in sides:
        peers, length = (lax.axis_size(axis), array.shape[dim])
        up = [(i, (i + 1) % peers) for i in range(peers)]
        last = lax.slice_in_dim(array, length - width, length, axis=dim)
        leading = lax.slice_in_dim(array, 0, width, axis=dim)
        edges[dim] = (
            lax.ppermute(last, axis, up),
            lax.ppermute(leading, axis, [(b, a) for a, b in up]),
        )
    done = []
    for _, dim in sides:
        low, high = edges[dim]
        around = [(width, width) if d in done else (0, 0) for d in range(array.ndim)]
        array = jnp.concatenate([jnp.pad(low, around), array, jnp.pad(high, around)], axis=dim)
        done.append(dim)
    return array


def padded_2(block, sides, width):
    for axis, dim in sides:
        count = lax.axis_size(axis)
        forward = [(i, i + 1) for i in range(count - 1)]
        backward = [(target, source) for source, target in forward]
        low = lax.ppermute(
            lax.slice_in_dim(block, block.shape[dim] - width, None, axis=dim), axis, forward
        )
        high = lax.ppermute(lax.slice_in_dim(block, 0, width, axis=dim), axis, backward)
        block = jnp.concatenate([low, block, high], axis=dim)
    return block


def by_axis(array, axes):
    for axis in axes:
        array = lax.psum(array, axis)
    return array


def lookup(classes, table):
    summed = jnp.zeros(classes.shape, jnp.float32)
    for level in range(table.shape[1]):
        summed = summed + jnp.where(
            classes == level, table[:, level][:, None, None], jnp.float32(0.0)
        )
    return summed


def harmonic(first, second):
    return 2.0 * first * second / (first + second)


def factor(diagonal, up_edge):
    inverses = []
    factors = []
    for level in range(diagonal.shape[0]):
        pivots = diagonal[level]
        if level > 0:
            pivots = pivots + up_edge[level - 1] * factors[level - 1]
        inverse = 1.0 / pivots
        inverses.append(inverse)
        factors.append(-up_edge[level] * inverse)
    return (jnp.stack(inverses), jnp.stack(factors))


def solve_block(inverses, factors, up_edge, source_term):
    forward = []
    for level in range(source_term.shape[0]):
        entries = source_term[level]
        if level > 0:
            entries = entries + up_edge[level - 1] * forward[level - 1]
        forward.append(entries * inverses[level])
    result = [forward[-1]]
    level = 0
    result.insert(0, forward[level] - factors[level] * result[0])
    return jnp.stack(result)


def plane_extend(field):
    return padded(field, ((GX, 2), (GY, 1)), 1)


def layer_extend(field):
    return padded_2(field, (("gz", 0),), 1)


def merged_sums(residual, precond, image_field):
    return (
        by_axis(jnp.sum(residual * precond), GX_GY_GZ),
        by_axis(jnp.sum(image_field * precond), GX_GY_GZ),
    )


def shards(load_current, sink_mask, pad_mask, plane_class, via_class, plane_table, via_table):
    n_layers, n_rows, n_cols = plane_class.shape
    g_plane = lookup(plane_class, plane_table)
    g_via = lookup(via_class, via_table)
    plane_ext = plane_extend(g_plane)
    middle = plane_ext[:, 1:-1, :]
    across = harmonic(middle[:, :, :-1], middle[:, :, 1:])
    east_edge = across[:, :, 1:]
    west_edge = across[:, :, :-1]
    column = plane_ext[:, :, 1:-1]
    along_rows = harmonic(column[:, :-1], column[:, 1:])
    north_edge = along_rows[:, 1:]
    south_edge = along_rows[:, :-1]
    via_ext = layer_extend(g_via)
    vertical = harmonic(via_ext[:-1], via_ext[1:])
    up_edge = vertical[1:]
    down_edge = vertical[:-1]
    group_index = lax.axis_index("gz")
    is_top = group_index == lax.axis_size("gz") - 1
    is_bottom = group_index == 0
    pad_plane = jnp.where(is_top, PAD_CONDUCTANCE * pad_mask.astype(jnp.float32), jnp.float32(0.0))
    pad_layer = jnp.concatenate(
        [jnp.zeros((n_layers - 1, n_rows, n_cols), jnp.float32), pad_plane[None]], 0
    )
    diagonal = east_edge + west_edge + north_edge + south_edge + up_edge + down_edge + pad_layer
    inverses, factors = factor(diagonal, up_edge)

    def precondition(residual):
        return solve_block(inverses, factors, up_edge, residual)

    def operate(field):
        inner = plane_extend(field)
        layer_ext = layer_extend(field)
        above_field = layer_ext[2:]
        below_field = layer_ext[:-2]
        return (
            diagonal * field
            - east_edge * inner[:, 1:-1, 2:]
            - west_edge * inner[:, 1:-1, :-2]
            - north_edge * inner[:, 2:, 1:-1]
            - south_edge * inner[:, :-2, 1:-1]
            - up_edge * above_field
            - down_edge * below_field
        )

    source = jnp.where(is_bottom, sink_mask.astype(jnp.float32) * load_current, jnp.float32(0.0))
    right_side = jnp.concatenate(
        [source[None], jnp.zeros((n_layers - 1, n_rows, n_cols), jnp.float32)], 0
    )
    voltage = jnp.zeros((n_layers, n_rows, n_cols), jnp.float32)
    residual = right_side
    precond = precondition(residual)
    image_field = operate(precond)
    weight_now, curvature = merged_sums(residual, precond, image_field)
    step_size = weight_now / curvature
    direction = precond
    image_dir = image_field
    for iteration in range(ITERS):
        voltage = voltage + step_size * direction
        residual = residual - step_size * image_dir
        if iteration + 1 < ITERS:
            precond = precondition(residual)
            image_field = operate(precond)
            weight_next, curvature = merged_sums(residual, precond, image_field)
            momentum = weight_next / weight_now
            step_size = weight_next / (curvature - momentum * weight_next / step_size)
            direction = precond + momentum * direction
            image_dir = image_field + momentum * image_dir
            weight_now = weight_next
    return (voltage, residual)


def solution(mesh):
    split = Mesh(
        mesh.devices.reshape(8, 2, 2, 4, mesh.shape["gz"]), ("gx_0", "gx_1", "gy_0", "gy_1", "gz")
    )
    placed = (
        P(GY, GX),
        P(GY, GX),
        P(GY, GX),
        P("gz", GY, GX),
        P("gz", GY, GX),
        P("gz", None),
        P("gz", None),
    )
    return jax.shard_map(
        shards,
        mesh=split,
        in_specs=placed,
        out_specs=(P("gz", GY, GX), P("gz", GY, GX)),
        check_vma=False,
    )
```

profile of v0, /device:TPU:32, one launch (start us, length us, event | category | flops | bytes accessed | tf_op | source)
XLA Modules:
  0.0 245.9 jit_solution(2650260789971561995)
XLA Ops:
  0.6 1.3 slice_reduce_fusion.15
  1.9 1.9 select_add_fusion.1
  3.8 1.7 collective-permute-start.2
  5.5 0.8 fusion.63
  6.2 1.7 collective-permute-start.1
  8.0 0.3 slice_reduce_fusion.7
  8.3 0.7 select_add_fusion
  9.0 0.9 fusion.64
  9.9 4.2 %collective-permute-start.4 = (f32[1,192,512]{2,1,0:T(8,128)}, f32[1,192,512]{2,1,0:T(8,128)}, u32[]{:S(2)}, u32[]{:S(2)}) collective-permute-start(f32[1,192,512]{2,1,0:T(8,128)} %get-tuple-element.79), channel_id=1, source_target_pairs={{0,1},{2,3},{4,5},{6,7},{8,9},{10,11},{12,13},{14,15},{16,17},{18,... | collective-permute-start | bytes 1179656 | tf_op jit(solution)/shard_map/ppermute | solution.py:39
  14.1 1.3 collective-permute-start.5
  15.5 4.7 %collective-permute-start.3 = (f32[2,1,512]{2,1,0:T(1,128)S(1)}, f32[2,1,512]{2,1,0:T(1,128)S(1)}, u32[]{:S(2)}, u32[]{:S(2)}) collective-permute-start(f32[2,1,512]{2,1,0:T(1,128)S(1)} %get-tuple-element.76), channel_id=1, source_target_pairs={{2,0},{4,2},{6,4},{8,6},{10,8},{12,10},{14,12},{0,14},{3,1},{5,3},... | collective-permute-start | bytes 12296 | tf_op jit(solution)/shard_map/ppermute | solution.py:23
  20.2 0.3 add_divide_fusion.1
  20.6 0.3 copy-done.19
  20.9 1.6 collective-permute-done.3
  22.5 1.3 add_divide_fusion.2
  23.7 3.6 %collective-permute-done.5 = f32[1,192,512]{2,1,0:T(8,128)} collective-permute-done((f32[1,192,512]{2,1,0:T(8,128)}, f32[1,192,512]{2,1,0:T(8,128)}, u32[]{:S(2)}, u32[]{:S(2)}) %collective-permute-start.5) | collective-permute-done | bytes 393248 | tf_op jit(solution)/shard_map/ppermute | solution.py:42
  27.3 1.3 add_divide_fusion
  28.7 0.4 pad_add_fusion
  29.1 0.6 copy-done.21
  29.7 0.1 copy-done.22
  29.8 0.2 fusion.56
  30.0 0.6 copy-done.1
  30.7 0.2 subtract_bitcast_fusion
  30.9 1.4 collective-permute-start.10
  32.3 4.6 %collective-permute-start.11 = (f32[1,192,512]{2,1,0:T(8,128)S(1)}, f32[1,192,512]{2,1,0:T(8,128)S(1)}, u32[]{:S(2)}, u32[]{:S(2)}) collective-permute-start(f32[1,192,512]{2,1,0:T(8,128)S(1)} %get-tuple-element.61), channel_id=1, source_target_pairs={{0,1},{2,3},{4,5},{6,7},{8,9},{10,11},{12,13},{14,15},{16,17},{18,... | collective-permute-start | bytes 1179656 | tf_op jit(solution)/shard_map/ppermute | solution.py:39
  36.9 4.9 %collective-permute-start.8 = (f32[2,1,512]{2,1,0:T(1,128)S(1)}, f32[2,1,512]{2,1,0:T(1,128)S(1)}, u32[]{:S(2)}, u32[]{:S(2)}) collective-permute-start(f32[2,1,512]{2,1,0:T(1,128)S(1)} %get-tuple-element.71), channel_id=1, source_target_pairs={{2,0},{4,2},{6,4},{8,6},{10,8},{12,10},{14,12},{0,14},{3,1},{5,3},... | collective-permute-start | bytes 12296 | tf_op jit(solution)/shard_map/ppermute | solution.py:23
  41.9 0.1 fusion.49
  42.0 5.1 %collective-permute-done.7 = f32[2,192,1]{2,1,0:T(8,128)S(1)} collective-permute-done((f32[2,192,1]{2,1,0:T(8,128)S(1)}, f32[2,192,1]{2,1,0:T(8,128)S(1)}, u32[]{:S(2)}, u32[]{:S(2)}) %collective-permute-start.7) | collective-permute-done | bytes 1568 | tf_op jit(solution)/shard_map/ppermute | solution.py:22
  47.1 3.2 %collective-permute-done.6 = f32[2,192,1]{2,1,0:T(8,128)S(1)} collective-permute-done((f32[2,192,1]{2,1,0:T(8,128)S(1)}, f32[2,192,1]{2,1,0:T(8,128)S(1)}, u32[]{:S(2)}, u32[]{:S(2)}) %collective-permute-start.6) | collective-permute-done | bytes 1568 | tf_op jit(solution)/shard_map/ppermute | solution.py:23
  50.3 3.1 %multiply_reduce_fusion.4 = (f32[]{:T(128)}, f32[]{:T(128)}, f32[2,192,512]{2,1,0:T(8,128)}) fusion(f32[1,192,512]{2,1,0:T(8,128)S(1)} %get-tuple-element.61, f32[1,192,512]{2,1,0:T(8,128)S(1)} %subtract_bitcast_fusion, f32[1,192,512]{2,1,0:T(8,128)S(1)} %bitcast.50, f32[1,192,512]{2,1,0:T(8,128)S(1)} %collective-permute-done.11, ...), kind=kLoop, calls=%fused_computation.135 | loop fusion | flops 8650750 | bytes 7875592 | tf_op jit(solution)/shard_map/reduce_sum | solution.py:103
  53.4 17.7 %all-reduce.12 = (f32[]{:T(128)}, f32[]{:T(128)}) all-reduce(f32[]{:T(128)} %get-tuple-element.7, f32[]{:T(128)} %get-tuple-element.6), channel_id=1, replica_groups=mesh['gx_0'=8,'gx_1'=2,'gy_0'=2,'gy_1'=4,'gz'=2] {'gx_0'}, use_global_device_ids=true, to_apply=%region_1.2 | all-reduce | flops 2 | bytes 16 | tf_op jit(solution)/shard_map/psum | solution.py:49
  71.1 3.1 %all-reduce.24 = (f32[]{:T(128)}, f32[]{:T(128)}) all-reduce(f32[]{:T(128)} %get-tuple-element.28, f32[]{:T(128)} %get-tuple-element.29), channel_id=1, replica_groups=mesh['gx_0'=8,'gx_1'=2,'gy_0'=2,'gy_1'=4,'gz'=2] {'gx_1'}, use_global_device_ids=true, to_apply=%region_2.3 | all-reduce | flops 2 | bytes 16 | tf_op jit(solution)/shard_map/psum | solution.py:49
  74.2 7.1 %all-reduce.21 = (f32[]{:T(128)}, f32[]{:T(128)}) all-reduce(f32[]{:T(128)} %get-tuple-element.52, f32[]{:T(128)} %get-tuple-element.53), channel_id=1, replica_groups=mesh['gx_0'=8,'gx_1'=2,'gy_0'=2,'gy_1'=4,'gz'=2] {'gy_0'}, use_global_device_ids=true, to_apply=%region_3.4 | all-reduce | flops 2 | bytes 16 | tf_op jit(solution)/shard_map/psum | solution.py:49
  81.3 12.6 %all-reduce.15 = (f32[]{:T(128)}, f32[]{:T(128)}) all-reduce(f32[]{:T(128)} %get-tuple-element.46, f32[]{:T(128)} %get-tuple-element.47), channel_id=1, replica_groups=mesh['gx_0'=8,'gx_1'=2,'gy_0'=2,'gy_1'=4,'gz'=2] {'gy_1'}, use_global_device_ids=true, to_apply=%region_4.5 | all-reduce | flops 2 | bytes 16 | tf_op jit(solution)/shard_map/psum | solution.py:49
  93.8 5.6 %all-reduce.18 = (f32[]{:T(128)}, f32[]{:T(128)}) all-reduce(f32[]{:T(128)} %get-tuple-element.34, f32[]{:T(128)} %get-tuple-element.35), channel_id=1, replica_groups=mesh['gx_0'=8,'gx_1'=2,'gy_0'=2,'gy_1'=4,'gz'=2] {'gz'}, use_global_device_ids=true, to_apply=%region_5.6 | all-reduce | flops 2 | bytes 16 | tf_op jit(solution)/shard_map/psum | solution.py:49
  100.7 1.3 pad_subtract_fusion
  102.1 0.2 multiply_subtract_fusion.3
  102.4 1.4 collective-permute-start.16
  103.8 4.6 %collective-permute-start.17 = (f32[1,192,512]{2,1,0:T(8,128)S(1)}, f32[1,192,512]{2,1,0:T(8,128)S(1)}, u32[]{:S(2)}, u32[]{:S(2)}) collective-permute-start(f32[1,192,512]{2,1,0:T(8,128)S(1)} %get-tuple-element.59), channel_id=1, source_target_pairs={{0,1},{2,3},{4,5},{6,7},{8,9},{10,11},{12,13},{14,15},{16,17},{18,... | collective-permute-start | bytes 1179656 | tf_op jit(solution)/shard_map/ppermute | solution.py:39
  108.4 1.3 collective-permute-start.14
  109.7 0.8 collective-permute-start.15
  110.7 5.1 %collective-permute-done.13 = f32[2,192,1]{2,1,0:T(8,128)S(1)} collective-permute-done((f32[2,192,1]{2,1,0:T(8,128)S(1)}, f32[2,192,1]{2,1,0:T(8,128)S(1)}, u32[]{:S(2)}, u32[]{:S(2)}) %collective-permute-start.13) | collective-permute-done | bytes 1568 | tf_op jit(solution)/shard_map/ppermute | solution.py:22
  115.8 3.2 %collective-permute-done.12 = f32[2,192,1]{2,1,0:T(8,128)S(1)} collective-permute-done((f32[2,192,1]{2,1,0:T(8,128)S(1)}, f32[2,192,1]{2,1,0:T(8,128)S(1)}, u32[]{:S(2)}, u32[]{:S(2)}) %collective-permute-start.12) | collective-permute-done | bytes 1568 | tf_op jit(solution)/shard_map/ppermute | solution.py:23
  119.0 3.2 %multiply_reduce_fusion.2 = (f32[]{:T(128)}, f32[]{:T(128)}, f32[2,192,512]{2,1,0:T(8,128)}) fusion(f32[1,192,512]{2,1,0:T(8,128)S(1)} %get-tuple-element.59, f32[1,192,512]{2,1,0:T(8,128)S(1)} %get-tuple-element.58, f32[1,192,512]{2,1,0:T(8,128)S(1)} %collective-permute-done.17, f32[1,192,512]{2,1,0:T(8,128)S(1)} %collective-permute-done.16, ...), kind=kLoop, calls=%fused_computation.133 | loop fusion | flops 9043966 | bytes 8662028 | tf_op jit(solution)/shard_map/reduce_sum | solution.py:103
  122.2 17.6 %all-reduce.11 = (f32[]{:T(128)}, f32[]{:T(128)}) all-reduce(f32[]{:T(128)} %get-tuple-element.5, f32[]{:T(128)} %get-tuple-element.4), channel_id=1, replica_groups=mesh['gx_0'=8,'gx_1'=2,'gy_0'=2,'gy_1'=4,'gz'=2] {'gx_0'}, use_global_device_ids=true, to_apply=%region_13.14 | all-reduce | flops 2 | bytes 16 | tf_op jit(solution)/shard_map/psum | solution.py:49
  139.8 3.3 %all-reduce.23 = (f32[]{:T(128)}, f32[]{:T(128)}) all-reduce(f32[]{:T(128)} %get-tuple-element.26, f32[]{:T(128)} %get-tuple-element.27), channel_id=1, replica_groups=mesh['gx_0'=8,'gx_1'=2,'gy_0'=2,'gy_1'=4,'gz'=2] {'gx_1'}, use_global_device_ids=true, to_apply=%region_14.15 | all-reduce | flops 2 | bytes 16 | tf_op jit(solution)/shard_map/psum | solution.py:49
  143.2 7.1 %all-reduce.20 = (f32[]{:T(128)}, f32[]{:T(128)}) all-reduce(f32[]{:T(128)} %get-tuple-element.50, f32[]{:T(128)} %get-tuple-element.51), channel_id=1, replica_groups=mesh['gx_0'=8,'gx_1'=2,'gy_0'=2,'gy_1'=4,'gz'=2] {'gy_0'}, use_global_device_ids=true, to_apply=%region_15.16 | all-reduce | flops 2 | bytes 16 | tf_op jit(solution)/shard_map/psum | solution.py:49
  150.2 11.8 %all-reduce.14 = (f32[]{:T(128)}, f32[]{:T(128)}) all-reduce(f32[]{:T(128)} %get-tuple-element.44, f32[]{:T(128)} %get-tuple-element.45), channel_id=1, replica_groups=mesh['gx_0'=8,'gx_1'=2,'gy_0'=2,'gy_1'=4,'gz'=2] {'gy_1'}, use_global_device_ids=true, to_apply=%region_16.17 | all-reduce | flops 2 | bytes 16 | tf_op jit(solution)/shard_map/psum | solution.py:49
  162.0 5.6 %all-reduce.17 = (f32[]{:T(128)}, f32[]{:T(128)}) all-reduce(f32[]{:T(128)} %get-tuple-element.32, f32[]{:T(128)} %get-tuple-element.33), channel_id=1, replica_groups=mesh['gx_0'=8,'gx_1'=2,'gy_0'=2,'gy_1'=4,'gz'=2] {'gz'}, use_global_device_ids=true, to_apply=%region_17.18 | all-reduce | flops 2 | bytes 16 | tf_op jit(solution)/shard_map/psum | solution.py:49
  172.0 1.7 multiply_subtract_fusion.1
  173.7 0.2 multiply_subtract_fusion.2
  174.0 1.4 collective-permute-start.22
  175.5 4.6 %collective-permute-start.23 = (f32[1,192,512]{2,1,0:T(8,128)S(1)}, f32[1,192,512]{2,1,0:T(8,128)S(1)}, u32[]{:S(2)}, u32[]{:S(2)}) collective-permute-start(f32[1,192,512]{2,1,0:T(8,128)S(1)} %get-tuple-element.56), channel_id=1, source_target_pairs={{0,1},{2,3},{4,5},{6,7},{8,9},{10,11},{12,13},{14,15},{16,17},{18,... | collective-permute-start | bytes 1179656 | tf_op jit(solution)/shard_map/ppermute | solution.py:39
  180.1 1.3 collective-permute-start.20
  181.4 0.8 collective-permute-start.21
  182.3 5.1 %collective-permute-done.19 = f32[2,192,1]{2,1,0:T(8,128)S(1)} collective-permute-done((f32[2,192,1]{2,1,0:T(8,128)S(1)}, f32[2,192,1]{2,1,0:T(8,128)S(1)}, u32[]{:S(2)}, u32[]{:S(2)}) %collective-permute-start.19) | collective-permute-done | bytes 1568 | tf_op jit(solution)/shard_map/ppermute | solution.py:22
  187.4 3.2 %collective-permute-done.18 = f32[2,192,1]{2,1,0:T(8,128)S(1)} collective-permute-done((f32[2,192,1]{2,1,0:T(8,128)S(1)}, f32[2,192,1]{2,1,0:T(8,128)S(1)}, u32[]{:S(2)}, u32[]{:S(2)}) %collective-permute-start.18) | collective-permute-done | bytes 1568 | tf_op jit(solution)/shard_map/ppermute | solution.py:23
  190.6 3.1 %multiply_reduce_fusion = (f32[]{:T(128)}, f32[]{:T(128)}, f32[2,192,512]{2,1,0:T(8,128)}) fusion(f32[1,192,512]{2,1,0:T(8,128)S(1)} %get-tuple-element.56, f32[1,192,512]{2,1,0:T(8,128)S(1)} %get-tuple-element.55, f32[2,192,512]{2,1,0:T(8,128)S(1)} %multiply_subtract_fusion.1, f32[1,192,512]{2,1,0:T(8,128)S(1)} %collective-permute-done.23, ...), kind=kLoop, calls=%fused_computation.129 | loop fusion | flops 8650750 | bytes 8268808 | tf_op jit(solution)/shard_map/reduce_sum | solution.py:103
  193.8 16.4 %all-reduce.10 = (f32[]{:T(128)}, f32[]{:T(128)}) all-reduce(f32[]{:T(128)} %get-tuple-element.3, f32[]{:T(128)} %get-tuple-element.2), channel_id=1, replica_groups=mesh['gx_0'=8,'gx_1'=2,'gy_0'=2,'gy_1'=4,'gz'=2] {'gx_0'}, use_global_device_ids=true, to_apply=%region_25.26 | all-reduce | flops 2 | bytes 16 | tf_op jit(solution)/shard_map/psum | solution.py:49
  210.2 3.1 %all-reduce.22 = (f32[]{:T(128)}, f32[]{:T(128)}) all-reduce(f32[]{:T(128)} %get-tuple-element.24, f32[]{:T(128)} %get-tuple-element.25), channel_id=1, replica_groups=mesh['gx_0'=8,'gx_1'=2,'gy_0'=2,'gy_1'=4,'gz'=2] {'gx_1'}, use_global_device_ids=true, to_apply=%region_26.27 | all-reduce | flops 2 | bytes 16 | tf_op jit(solution)/shard_map/psum | solution.py:49
  213.3 7.1 %all-reduce.19 = (f32[]{:T(128)}, f32[]{:T(128)}) all-reduce(f32[]{:T(128)} %get-tuple-element.48, f32[]{:T(128)} %get-tuple-element.49), channel_id=1, replica_groups=mesh['gx_0'=8,'gx_1'=2,'gy_0'=2,'gy_1'=4,'gz'=2] {'gy_0'}, use_global_device_ids=true, to_apply=%region_27.28 | all-reduce | flops 2 | bytes 16 | tf_op jit(solution)/shard_map/psum | solution.py:49
  220.4 11.7 %all-reduce.13 = (f32[]{:T(128)}, f32[]{:T(128)}) all-reduce(f32[]{:T(128)} %get-tuple-element.42, f32[]{:T(128)} %get-tuple-element.43), channel_id=1, replica_groups=mesh['gx_0'=8,'gx_1'=2,'gy_0'=2,'gy_1'=4,'gz'=2] {'gy_1'}, use_global_device_ids=true, to_apply=%region_28.29 | all-reduce | flops 2 | bytes 16 | tf_op jit(solution)/shard_map/psum | solution.py:49
  232.1 5.6 %all-reduce.16 = (f32[]{:T(128)}, f32[]{:T(128)}) all-reduce(f32[]{:T(128)} %get-tuple-element.30, f32[]{:T(128)} %get-tuple-element.31), channel_id=1, replica_groups=mesh['gx_0'=8,'gx_1'=2,'gy_0'=2,'gy_1'=4,'gz'=2] {'gz'}, use_global_device_ids=true, to_apply=%region_29.30 | all-reduce | flops 2 | bytes 16 | tf_op jit(solution)/shard_map/psum | solution.py:49
  241.5 4.4 %multiply_subtract_fusion = (f32[2,192,512]{2,1,0:T(8,128)}, f32[2,192,512]{2,1,0:T(8,128)}) fusion(f32[2,192,512]{2,1,0:T(8,128)} %copy-done.4, f32[2,192,512]{2,1,0:T(8,128)} %get-tuple-element.54, f32[]{:T(128)S(6)} %div.60, f32[]{:T(128)S(6)} %div.62, f32[2,192,512]{2,1,0:T(8,128)} %get-tuple-element.57, f32[2,192,512]{2,1,0:T(8,128)} %get-tuple-element.60, ...), kind=kLoop, calls=%fused_computation.127 | loop fusion | flops 3538944 | bytes 7077908 | tf_op jit(solution)/shard_map/sub | solution.py:166
  (75 shorter events, 0.6 us)
Async XLA Ops:
  1.9 6.1 %copy-start.23 = (f32[2,8]{1,0:T(2,128)S(1)}, f32[2,8]{1,0:T(2,128)}, u32[]{:S(2)}) copy-start(f32[2,8]{1,0:T(2,128)} %param.13) | copy-start | bytes 196
  1.9 6.4 %copy-start.17 = (s32[2,192,512]{2,1,0:T(8,128)S(1)}, s32[2,192,512]{2,1,0:T(8,128)}, u32[]{:S(2)}) copy-start(s32[2,192,512]{2,1,0:T(8,128)} %param.11) | copy-start | bytes 2359300
  3.8 16.8 %collective-permute-start.2 = (f32[2,1,512]{2,1,0:T(1,128)S(1)}, f32[2,1,512]{2,1,0:T(1,128)S(1)}, u32[]{:S(2)}, u32[]{:S(2)}) collective-permute-start(f32[2,1,512]{2,1,0:T(1,128)S(1)} %get-tuple-element.75), channel_id=1, source_target_pairs={{0,2},{2,4},{4,6},{6,8},{8,10},{10,12},{12,14},{14,0},{1,3},{3,5},... | collective-permute-start | bytes 12296 | tf_op jit(solution)/shard_map/ppermute | solution.py:22
  6.2 9.2 %collective-permute-start = (f32[2,192,1]{2,1,0:T(8,128)}, f32[2,192,1]{2,1,0:T(8,128)S(1)}, u32[]{:S(2)}, u32[]{:S(2)}) collective-permute-start(f32[2,192,1]{2,1,0:T(8,128)} %get-tuple-element.77), channel_id=1, source_target_pairs={{0,16},{16,32},{32,48},{48,64},{64,80},{80,96},{96,112},{112,128},... | collective-permute-start | bytes 4616 | tf_op jit(solution)/shard_map/ppermute | solution.py:22
  6.2 14.0 %collective-permute-start.1 = (f32[2,192,1]{2,1,0:T(8,128)S(1)}, f32[2,192,1]{2,1,0:T(8,128)S(1)}, u32[]{:S(2)}, u32[]{:S(2)}) collective-permute-start(f32[2,192,1]{2,1,0:T(8,128)S(1)} %get-tuple-element.78), channel_id=1, source_target_pairs={{16,0},{32,16},{48,32},{64,48},{80,64},{96,80},{112,96},{128,112},... | collective-permute-start | bytes 4616 | tf_op jit(solution)/shard_map/ppermute | solution.py:23
  8.9 6.4 %copy-start.15 = (f32[2,192,512]{2,1,0:T(8,128)}, f32[2,192,512]{2,1,0:T(8,128)S(1)}, u32[]{:S(2)}) copy-start(f32[2,192,512]{2,1,0:T(8,128)S(1)} %select_add_fusion) | copy-start | bytes 2359300
  9.0 6.4 %copy-start.20 = (s32[192,512]{1,0:T(8,128)S(1)}, s32[192,512]{1,0:T(8,128)}, u32[]{:S(2)}) copy-start(s32[192,512]{1,0:T(8,128)} %param.9) | copy-start | bytes 1179652
  9.9 13.8 %collective-permute-start.4 = (f32[1,192,512]{2,1,0:T(8,128)}, f32[1,192,512]{2,1,0:T(8,128)}, u32[]{:S(2)}, u32[]{:S(2)}) collective-permute-start(f32[1,192,512]{2,1,0:T(8,128)} %get-tuple-element.79), channel_id=1, source_target_pairs={{0,1},{2,3},{4,5},{6,7},{8,9},{10,11},{12,13},{14,15},{16,17},{18,... | collective-permute-start | bytes 1179656 | tf_op jit(solution)/shard_map/ppermute | solution.py:39
  14.1 13.3 %collective-permute-start.5 = (f32[1,192,512]{2,1,0:T(8,128)}, f32[1,192,512]{2,1,0:T(8,128)}, u32[]{:S(2)}, u32[]{:S(2)}) collective-permute-start(f32[1,192,512]{2,1,0:T(8,128)} %get-tuple-element.80), channel_id=1, source_target_pairs={{1,0},{3,2},{5,4},{7,6},{9,8},{11,10},{13,12},{15,14},{17,16},{19,... | collective-permute-start | bytes 1179656 | tf_op jit(solution)/shard_map/ppermute | solution.py:42
  15.4 13.2 %copy-start.5 = (f32[1,192,512]{2,1,0:T(8,128)}, f32[1,192,512]{2,1,0:T(8,128)S(1)}, u32[]{:S(2)}) copy-start(f32[1,192,512]{2,1,0:T(8,128)S(1)} %select_bitcast_fusion) | copy-start | bytes 1179652
  15.4 5.1 %copy-start.18 = (f32[2,192,1]{2,1,0:T(8,128)}, f32[2,192,1]{2,1,0:T(8,128)S(1)}, u32[]{:S(2)}) copy-start(f32[2,192,1]{2,1,0:T(8,128)S(1)} %collective-permute-done) | copy-start | bytes 4612
  15.5 7.0 %collective-permute-start.3 = (f32[2,1,512]{2,1,0:T(1,128)S(1)}, f32[2,1,512]{2,1,0:T(1,128)S(1)}, u32[]{:S(2)}, u32[]{:S(2)}) collective-permute-start(f32[2,1,512]{2,1,0:T(1,128)S(1)} %get-tuple-element.76), channel_id=1, source_target_pairs={{2,0},{4,2},{6,4},{8,6},{10,8},{12,10},{14,12},{0,14},{3,1},{5,3},... | collective-permute-start | bytes 12296 | tf_op jit(solution)/shard_map/ppermute | solution.py:23
  20.2 0.7 copy-start.19
  20.5 6.8 %copy-start.16 = (f32[2,192,512]{2,1,0:T(8,128)S(1)}, f32[2,192,512]{2,1,0:T(8,128)}, u32[]{:S(2)}) copy-start(f32[2,192,512]{2,1,0:T(8,128)} %copy-done.15) | copy-start | bytes 2359300
  28.7 1.0 copy-start.21
  28.7 1.1 copy-start.22
  29.8 0.9 copy-start.1
  30.0 20.3 %copy-start.9 = (f32[1,192,512]{2,1,0:T(8,128)}, f32[1,192,512]{2,1,0:T(8,128)S(1)}, u32[]{:S(2)}) copy-start(f32[1,192,512]{2,1,0:T(8,128)S(1)} %get-tuple-element.61) | copy-start | bytes 1179652
  30.9 22.6 %copy-start.10 = (f32[1,192,512]{2,1,0:T(8,128)}, f32[1,192,512]{2,1,0:T(8,128)S(1)}, u32[]{:S(2)}) copy-start(f32[1,192,512]{2,1,0:T(8,128)S(1)} %subtract_bitcast_fusion) | copy-start | bytes 1179652
  30.9 19.4 %copy-start.6 = (f32[1,192,512]{2,1,0:T(8,128)S(1)}, f32[1,192,512]{2,1,0:T(8,128)}, u32[]{:S(2)}) copy-start(f32[1,192,512]{2,1,0:T(8,128)} %copy-done.5) | copy-start | bytes 1179652
  30.9 19.4 %collective-permute-start.10 = (f32[1,192,512]{2,1,0:T(8,128)S(1)}, f32[1,192,512]{2,1,0:T(8,128)S(1)}, u32[]{:S(2)}, u32[]{:S(2)}) collective-permute-start(f32[1,192,512]{2,1,0:T(8,128)S(1)} %subtract_bitcast_fusion), channel_id=1, source_target_pairs={{1,0},{3,2},{5,4},{7,6},{9,8},{11,10},{13,12},{15,14},{17,16},{19,... | collective-permute-start | bytes 1179656 | tf_op jit(solution)/shard_map/ppermute | solution.py:42
  32.3 18.0 %collective-permute-start.11 = (f32[1,192,512]{2,1,0:T(8,128)S(1)}, f32[1,192,512]{2,1,0:T(8,128)S(1)}, u32[]{:S(2)}, u32[]{:S(2)}) collective-permute-start(f32[1,192,512]{2,1,0:T(8,128)S(1)} %get-tuple-element.61), channel_id=1, source_target_pairs={{0,1},{2,3},{4,5},{6,7},{8,9},{10,11},{12,13},{14,15},{16,17},{18,... | collective-permute-start | bytes 1179656 | tf_op jit(solution)/shard_map/ppermute | solution.py:39
  36.9 13.4 %collective-permute-start.8 = (f32[2,1,512]{2,1,0:T(1,128)S(1)}, f32[2,1,512]{2,1,0:T(1,128)S(1)}, u32[]{:S(2)}, u32[]{:S(2)}) collective-permute-start(f32[2,1,512]{2,1,0:T(1,128)S(1)} %get-tuple-element.71), channel_id=1, source_target_pairs={{2,0},{4,2},{6,4},{8,6},{10,8},{12,10},{14,12},{0,14},{3,1},{5,3},... | collective-permute-start | bytes 12296 | tf_op jit(solution)/shard_map/ppermute | solution.py:23
  41.8 8.4 %collective-permute-start.9 = (f32[2,1,512]{2,1,0:T(1,128)S(1)}, f32[2,1,512]{2,1,0:T(1,128)S(1)}, u32[]{:S(2)}, u32[]{:S(2)}) collective-permute-start(f32[2,1,512]{2,1,0:T(1,128)S(1)} %get-tuple-element.72), channel_id=1, source_target_pairs={{0,2},{2,4},{4,6},{6,8},{8,10},{10,12},{12,14},{14,0},{1,3},{3,5},... | collective-permute-start | bytes 12296 | tf_op jit(solution)/shard_map/ppermute | solution.py:22
  42.0 5.1 %collective-permute-start.7 = (f32[2,192,1]{2,1,0:T(8,128)S(1)}, f32[2,192,1]{2,1,0:T(8,128)S(1)}, u32[]{:S(2)}, u32[]{:S(2)}) collective-permute-start(f32[2,192,1]{2,1,0:T(8,128)S(1)} %get-tuple-element.73), channel_id=1, source_target_pairs={{0,16},{16,32},{32,48},{48,64},{64,80},{80,96},{96,112},{112,128},... | collective-permute-start | bytes 4616 | tf_op jit(solution)/shard_map/ppermute | solution.py:22
  47.1 3.2 %collective-permute-start.6 = (f32[2,192,1]{2,1,0:T(8,128)S(1)}, f32[2,192,1]{2,1,0:T(8,128)S(1)}, u32[]{:S(2)}, u32[]{:S(2)}) collective-permute-start(f32[2,192,1]{2,1,0:T(8,128)S(1)} %get-tuple-element.74), channel_id=1, source_target_pairs={{16,0},{32,16},{48,32},{64,48},{80,64},{96,80},{112,96},{128,112},... | collective-permute-start | bytes 4616 | tf_op jit(solution)/shard_map/ppermute | solution.py:23
  100.7 1.4 copy-start.2
  102.3 19.9 %copy-start.11 = (f32[1,192,512]{2,1,0:T(8,128)}, f32[1,192,512]{2,1,0:T(8,128)S(1)}, u32[]{:S(2)}) copy-start(f32[1,192,512]{2,1,0:T(8,128)S(1)} %get-tuple-element.58) | copy-start | bytes 1179652
  102.3 19.9 %copy-start.12 = (f32[1,192,512]{2,1,0:T(8,128)}, f32[1,192,512]{2,1,0:T(8,128)S(1)}, u32[]{:S(2)}) copy-start(f32[1,192,512]{2,1,0:T(8,128)S(1)} %get-tuple-element.59) | copy-start | bytes 1179652
  102.4 16.6 %copy-start = (f32[2,192,512]{2,1,0:T(8,128)S(1)}, f32[2,192,512]{2,1,0:T(8,128)}, u32[]{:S(2)}) copy-start(f32[2,192,512]{2,1,0:T(8,128)} %get-tuple-element.60) | copy-start | bytes 2359300
  102.4 16.6 %copy-start.7 = (f32[1,192,512]{2,1,0:T(8,128)S(1)}, f32[1,192,512]{2,1,0:T(8,128)}, u32[]{:S(2)}) copy-start(f32[1,192,512]{2,1,0:T(8,128)} %copy-done.5) | copy-start | bytes 1179652
  102.4 16.6 %collective-permute-start.16 = (f32[1,192,512]{2,1,0:T(8,128)S(1)}, f32[1,192,512]{2,1,0:T(8,128)S(1)}, u32[]{:S(2)}, u32[]{:S(2)}) collective-permute-start(f32[1,192,512]{2,1,0:T(8,128)S(1)} %get-tuple-element.58), channel_id=1, source_target_pairs={{1,0},{3,2},{5,4},{7,6},{9,8},{11,10},{13,12},{15,14},{17,16},{19,... | collective-permute-start | bytes 1179656 | tf_op jit(solution)/shard_map/ppermute | solution.py:42
  103.8 15.2 %collective-permute-start.17 = (f32[1,192,512]{2,1,0:T(8,128)S(1)}, f32[1,192,512]{2,1,0:T(8,128)S(1)}, u32[]{:S(2)}, u32[]{:S(2)}) collective-permute-start(f32[1,192,512]{2,1,0:T(8,128)S(1)} %get-tuple-element.59), channel_id=1, source_target_pairs={{0,1},{2,3},{4,5},{6,7},{8,9},{10,11},{12,13},{14,15},{16,17},{18,... | collective-permute-start | bytes 1179656 | tf_op jit(solution)/shard_map/ppermute | solution.py:39
  108.4 10.5 %collective-permute-start.14 = (f32[2,1,512]{2,1,0:T(1,128)S(1)}, f32[2,1,512]{2,1,0:T(1,128)S(1)}, u32[]{:S(2)}, u32[]{:S(2)}) collective-permute-start(f32[2,1,512]{2,1,0:T(1,128)S(1)} %get-tuple-element.67), channel_id=1, source_target_pairs={{2,0},{4,2},{6,4},{8,6},{10,8},{12,10},{14,12},{0,14},{3,1},{5,3},... | collective-permute-start | bytes 12296 | tf_op jit(solution)/shard_map/ppermute | solution.py:23
  109.7 9.3 %collective-permute-start.15 = (f32[2,1,512]{2,1,0:T(1,128)S(1)}, f32[2,1,512]{2,1,0:T(1,128)S(1)}, u32[]{:S(2)}, u32[]{:S(2)}) collective-permute-start(f32[2,1,512]{2,1,0:T(1,128)S(1)} %get-tuple-element.68), channel_id=1, source_target_pairs={{0,2},{2,4},{4,6},{6,8},{8,10},{10,12},{12,14},{14,0},{1,3},{3,5},... | collective-permute-start | bytes 12296 | tf_op jit(solution)/shard_map/ppermute | solution.py:22
  110.6 5.1 %collective-permute-start.13 = (f32[2,192,1]{2,1,0:T(8,128)S(1)}, f32[2,192,1]{2,1,0:T(8,128)S(1)}, u32[]{:S(2)}, u32[]{:S(2)}) collective-permute-start(f32[2,192,1]{2,1,0:T(8,128)S(1)} %get-tuple-element.69), channel_id=1, source_target_pairs={{0,16},{16,32},{32,48},{48,64},{64,80},{80,96},{96,112},{112,128},... | collective-permute-start | bytes 4616 | tf_op jit(solution)/shard_map/ppermute | solution.py:22
  115.8 3.2 %collective-permute-start.12 = (f32[2,192,1]{2,1,0:T(8,128)S(1)}, f32[2,192,1]{2,1,0:T(8,128)S(1)}, u32[]{:S(2)}, u32[]{:S(2)}) collective-permute-start(f32[2,192,1]{2,1,0:T(8,128)S(1)} %get-tuple-element.70), channel_id=1, source_target_pairs={{16,0},{32,16},{48,32},{64,48},{80,64},{96,80},{112,96},{128,112},... | collective-permute-start | bytes 4616 | tf_op jit(solution)/shard_map/ppermute | solution.py:23
  172.0 1.7 copy-start.3
  173.7 16.9 %copy-start.4 = (f32[2,192,512]{2,1,0:T(8,128)}, f32[2,192,512]{2,1,0:T(8,128)S(1)}, u32[]{:S(2)}) copy-start(f32[2,192,512]{2,1,0:T(8,128)S(1)} %multiply_subtract_fusion.1) | copy-start | bytes 2359300
  174.0 19.8 %copy-start.13 = (f32[1,192,512]{2,1,0:T(8,128)}, f32[1,192,512]{2,1,0:T(8,128)S(1)}, u32[]{:S(2)}) copy-start(f32[1,192,512]{2,1,0:T(8,128)S(1)} %get-tuple-element.55) | copy-start | bytes 1179652
  174.0 19.8 %copy-start.14 = (f32[1,192,512]{2,1,0:T(8,128)}, f32[1,192,512]{2,1,0:T(8,128)S(1)}, u32[]{:S(2)}) copy-start(f32[1,192,512]{2,1,0:T(8,128)S(1)} %get-tuple-element.56) | copy-start | bytes 1179652
  174.0 16.6 %copy-start.8 = (f32[1,192,512]{2,1,0:T(8,128)S(1)}, f32[1,192,512]{2,1,0:T(8,128)}, u32[]{:S(2)}) copy-start(f32[1,192,512]{2,1,0:T(8,128)} %copy-done.5) | copy-start | bytes 1179652
  174.0 16.6 %collective-permute-start.22 = (f32[1,192,512]{2,1,0:T(8,128)S(1)}, f32[1,192,512]{2,1,0:T(8,128)S(1)}, u32[]{:S(2)}, u32[]{:S(2)}) collective-permute-start(f32[1,192,512]{2,1,0:T(8,128)S(1)} %get-tuple-element.55), channel_id=1, source_target_pairs={{1,0},{3,2},{5,4},{7,6},{9,8},{11,10},{13,12},{15,14},{17,16},{19,... | collective-permute-start | bytes 1179656 | tf_op jit(solution)/shard_map/ppermute | solution.py:42
  175.5 15.2 %collective-permute-start.23 = (f32[1,192,512]{2,1,0:T(8,128)S(1)}, f32[1,192,512]{2,1,0:T(8,128)S(1)}, u32[]{:S(2)}, u32[]{:S(2)}) collective-permute-start(f32[1,192,512]{2,1,0:T(8,128)S(1)} %get-tuple-element.56), channel_id=1, source_target_pairs={{0,1},{2,3},{4,5},{6,7},{8,9},{10,11},{12,13},{14,15},{16,17},{18,... | collective-permute-start | bytes 1179656 | tf_op jit(solution)/shard_map/ppermute | solution.py:39
  180.1 10.5 %collective-permute-start.20 = (f32[2,1,512]{2,1,0:T(1,128)S(1)}, f32[2,1,512]{2,1,0:T(1,128)S(1)}, u32[]{:S(2)}, u32[]{:S(2)}) collective-permute-start(f32[2,1,512]{2,1,0:T(1,128)S(1)} %get-tuple-element.63), channel_id=1, source_target_pairs={{2,0},{4,2},{6,4},{8,6},{10,8},{12,10},{14,12},{0,14},{3,1},{5,3},... | collective-permute-start | bytes 12296 | tf_op jit(solution)/shard_map/ppermute | solution.py:23
  181.4 9.2 %collective-permute-start.21 = (f32[2,1,512]{2,1,0:T(1,128)S(1)}, f32[2,1,512]{2,1,0:T(1,128)S(1)}, u32[]{:S(2)}, u32[]{:S(2)}) collective-permute-start(f32[2,1,512]{2,1,0:T(1,128)S(1)} %get-tuple-element.64), channel_id=1, source_target_pairs={{0,2},{2,4},{4,6},{6,8},{8,10},{10,12},{12,14},{14,0},{1,3},{3,5},... | collective-permute-start | bytes 12296 | tf_op jit(solution)/shard_map/ppermute | solution.py:22
  182.3 5.1 %collective-permute-start.19 = (f32[2,192,1]{2,1,0:T(8,128)S(1)}, f32[2,192,1]{2,1,0:T(8,128)S(1)}, u32[]{:S(2)}, u32[]{:S(2)}) collective-permute-start(f32[2,192,1]{2,1,0:T(8,128)S(1)} %get-tuple-element.65), channel_id=1, source_target_pairs={{0,16},{16,32},{32,48},{48,64},{64,80},{80,96},{96,112},{112,128},... | collective-permute-start | bytes 4616 | tf_op jit(solution)/shard_map/ppermute | solution.py:22
  187.4 3.2 %collective-permute-start.18 = (f32[2,192,1]{2,1,0:T(8,128)S(1)}, f32[2,192,1]{2,1,0:T(8,128)S(1)}, u32[]{:S(2)}, u32[]{:S(2)}) collective-permute-start(f32[2,192,1]{2,1,0:T(8,128)S(1)} %get-tuple-element.66), channel_id=1, source_target_pairs={{16,0},{32,16},{48,32},{64,48},{80,64},{96,80},{112,96},{128,112},... | collective-permute-start | bytes 4616 | tf_op jit(solution)/shard_map/ppermute | solution.py:23
where the time goes:
time: 247 us; the launch traced here: 246 us
  blocking collectives  135 us (55%)
  starting transfers between devices  40.8 us (17%)
  waiting for transfers between devices  30 us (12%)
  other arithmetic  23.9 us (10%)
  between operations  10.7 us (4%)
  local copies, waits for them, and re-layouts  5.05 us (2%)
    psum x15, blocking collectives, by_axis(): array = lax.psum(array, axis)  135 us
    ppermute x4, starting transfers between devices, padded_2(): lax.ppermute(lax.slice_in_dim(block, block.shape[dim] - width, None, axis...  17.9 us
    ppermute x8, waiting for transfers between devices, padded(): lax.ppermute(last, axis, up)  15.3 us
    ppermute x8, starting transfers between devices, padded(): lax.ppermute(leading, axis, [(b, a) for a, b in up])  14 us
    ppermute x8, waiting for transfers between devices, padded(): lax.ppermute(leading, axis, [(b, a) for a, b in up])  11.2 us
    reduce_sum x3, other arithmetic, merged_sums(): jnp.sum(image_field * precond)  9.43 us
    sub x3, other arithmetic, shards(): residual = residual - step_size * image_dir  7.35 us
    ppermute x4, starting transfers between devices, padded_2(): lax.ppermute(lax.slice_in_dim(block, 0, width, axis=dim), axis, backward)  5.55 us
  transfers between devices with their start and end apart: 24, of which 8 were waited for; matrix products, arithmetic and copies ran while one was open for 2% of the time, Pallas kernels for 0%

commit v1 on v0

--- a/solution.py
+++ b/solution.py
@@ -46,7 +46,7 @@
 
 def by_axis(array, axes):
     for axis in axes:
-        array = lax.psum(array, axis)
+        array = jnp.sum(lax.all_gather(array, axis), axis=0)
     return array
 
 

time: 247 us -> 309 us (1.25)
  local copies, waits for them, and re-layouts: 5.05 us -> 48.2 us
  other arithmetic: 23.9 us -> 50.3 us
  blocking collectives: 135 us -> 125 us
  starting transfers between devices: 40.8 us -> 46.7 us
  waiting for transfers between devices: 30 us -> 26.5 us
    psum x15 -> x0, blocking collectives: 135 us -> none  [by_axis(): array = lax.psum(array, axis)]
    unnamed x0 -> x15, blocking collectives: none -> 125 us
    unnamed x48 -> x119, local copies, waits for them, and re-layouts: 1.78 us -> 44.9 us
    reduce_sum x0 -> x30, other arithmetic: none -> 19 us  [by_axis(): array = jnp.sum(lax.all_gather(array, axis), axis=0)]
    ppermute x8, starting transfers between devices: 3.36 us -> 7.67 us  [padded(): lax.ppermute(last, axis, up)]
    another operation x8, other arithmetic: 0.79 us -> 4.81 us  [solve_block(): return jnp.stack(result)]
    reduce_sum x3, other arithmetic: 9.43 us -> 12.8 us  [merged_sums(): jnp.sum(image_field * precond)]
    ppermute x8, waiting for transfers between devices: 15.3 us -> 12.1 us  [padded(): lax.ppermute(last, axis, up)]
where the time goes in v1:
time: 309 us; the launch traced here: 308 us
  blocking collectives  125 us (40%)
  other arithmetic  50.3 us (16%)
  local copies, waits for them, and re-layouts  48.2 us (16%)
  starting transfers between devices  46.7 us (15%)
  waiting for transfers between devices  26.5 us (9%)
  between operations  10.7 us (3%)
    unnamed x15, blocking collectives  125 us
    unnamed x119, local copies, waits for them, and re-layouts  44.9 us
    ppermute x4, starting transfers between devices, padded_2(): lax.ppermute(lax.slice_in_dim(block, block.shape[dim] - width, None, axis...  19.4 us
    reduce_sum x30, other arithmetic, by_axis(): array = jnp.sum(lax.all_gather(array, axis), axis=0)  19 us
    ppermute x8, starting transfers between devices, padded(): lax.ppermute(leading, axis, [(b, a) for a, b in up])  14.1 us
    reduce_sum x3, other arithmetic, merged_sums(): jnp.sum(image_field * precond)  12.8 us
    ppermute x8, waiting for transfers between devices, padded(): lax.ppermute(last, axis, up)  12.1 us
    ppermute x8, waiting for transfers between devices, padded(): lax.ppermute(leading, axis, [(b, a) for a, b in up])  10.9 us
  transfers between devices with their start and end apart: 24, of which 8 were waited for; matrix products, arithmetic and copies ran while one was open for 2% of the time, Pallas kernels for 0%

profile of v1, /device:TPU:32, one launch (start us, length us, event | category | flops | bytes accessed | tf_op | source)
XLA Modules:
  0.0 307.6 jit_solution(2699617702233151919)
XLA Ops:
  1.9 1.9 select_add_fusion.1
  4.6 1.7 collective-permute-start.1
  6.3 1.6 collective-permute-start.2
  9.9 4.2 %collective-permute-start.4 = (f32[1,192,512]{2,1,0:T(8,128)}, f32[1,192,512]{2,1,0:T(8,128)}, u32[]{:S(2)}, u32[]{:S(2)}) collective-permute-start(f32[1,192,512]{2,1,0:T(8,128)} %get-tuple-element.79), channel_id=1, source_target_pairs={{0,1},{2,3},{4,5},{6,7},{8,9},{10,11},{12,13},{14,15},{16,17},{18,... | collective-permute-start | bytes 1179656 | tf_op jit(solution)/shard_map/ppermute | solution.py:39
  15.4 4.7 %collective-permute-start.3 = (f32[2,1,512]{2,1,0:T(1,128)S(1)}, f32[2,1,512]{2,1,0:T(1,128)S(1)}, u32[]{:S(2)}, u32[]{:S(2)}) collective-permute-start(f32[2,1,512]{2,1,0:T(1,128)S(1)} %get-tuple-element.76), channel_id=1, source_target_pairs={{2,0},{4,2},{6,4},{8,6},{10,8},{12,10},{14,12},{0,14},{3,1},{5,3},... | collective-permute-start | bytes 12296 | tf_op jit(solution)/shard_map/ppermute | solution.py:23
  23.5 3.6 %collective-permute-done.5 = f32[1,192,512]{2,1,0:T(8,128)} collective-permute-done((f32[1,192,512]{2,1,0:T(8,128)}, f32[1,192,512]{2,1,0:T(8,128)}, u32[]{:S(2)}, u32[]{:S(2)}) %collective-permute-start.5) | collective-permute-done | bytes 393248 | tf_op jit(solution)/shard_map/ppermute | solution.py:42
  31.5 1.4 collective-permute-start.10
  32.9 6.1 %collective-permute-start.11 = (f32[1,192,512]{2,1,0:T(8,128)}, f32[1,192,512]{2,1,0:T(8,128)}, u32[]{:S(2)}, u32[]{:S(2)}) collective-permute-start(f32[1,192,512]{2,1,0:T(8,128)} %get-tuple-element.61), channel_id=1, source_target_pairs={{0,1},{2,3},{4,5},{6,7},{8,9},{10,11},{12,13},{14,15},{16,17},{18,... | collective-permute-start | bytes 1179656 | tf_op jit(solution)/shard_map/ppermute | solution.py:39
  39.7 4.9 %collective-permute-start.8 = (f32[2,1,512]{2,1,0:T(1,128)S(1)}, f32[2,1,512]{2,1,0:T(1,128)S(1)}, u32[]{:S(2)}, u32[]{:S(2)}) collective-permute-start(f32[2,1,512]{2,1,0:T(1,128)S(1)} %get-tuple-element.71), channel_id=1, source_target_pairs={{2,0},{4,2},{6,4},{8,6},{10,8},{12,10},{14,12},{0,14},{3,1},{5,3},... | collective-permute-start | bytes 12296 | tf_op jit(solution)/shard_map/ppermute | solution.py:23
  44.6 1.8 fusion.49
  46.5 3.2 %collective-permute-done.6 = f32[2,192,1]{2,1,0:T(8,128)S(1)} collective-permute-done((f32[2,192,1]{2,1,0:T(8,128)S(1)}, f32[2,192,1]{2,1,0:T(8,128)S(1)}, u32[]{:S(2)}, u32[]{:S(2)}) %collective-permute-start.6) | collective-permute-done | bytes 1568 | tf_op jit(solution)/shard_map/ppermute | solution.py:23
  50.3 2.3 collective-permute-start.7
  53.2 3.0 collective-permute-done.7
  56.3 6.4 %multiply_reduce_fusion.4 = (f32[]{:T(128)}, f32[]{:T(128)}, f32[2,192,512]{2,1,0:T(8,128)}) fusion(f32[1,192,512]{2,1,0:T(8,128)} %get-tuple-element.61, f32[1,192,512]{2,1,0:T(8,128)} %subtract_bitcast_fusion, f32[1,192,512]{2,1,0:T(8,128)S(1)} %bitcast.85, f32[1,192,512]{2,1,0:T(8,128)} %collective-permute-done.11, ...), kind=kLoop, calls=%fused_computation.135 | loop fusion | flops 8650750 | bytes 7875592 | tf_op jit(solution)/shard_map/reduce_sum | solution.py:103
  62.7 1.4 dynamic-update-slice
  66.0 18.2 %all-reduce.42 = (f32[8]{0:T(128)S(1)}, f32[8]{0:T(128)S(1)}) all-reduce(f32[8]{0:T(128)S(1)} %dynamic-update-slice, f32[8]{0:T(128)S(1)} %dynamic-update-slice.5), channel_id=1, replica_groups=mesh['gx_0'=8,'gx_1'=2,'gy_0'=2,'gy_1'=4,'gz'=2] {'gx_0'}, use_global_device_ids=true, to_apply=%add.10 | all-reduce | flops 16 | bytes 128
  85.5 1.3 dynamic-update-slice.6
  86.8 1.3 dynamic-update-slice.1
  88.7 2.4 all-reduce.54
  92.5 1.4 dynamic-update-slice.7
  93.8 1.4 dynamic-update-slice.2
  95.8 6.4 %all-reduce.51 = (f32[2]{0:T(128)S(1)}, f32[2]{0:T(128)S(1)}) all-reduce(f32[2]{0:T(128)S(1)} %dynamic-update-slice.2, f32[2]{0:T(128)S(1)} %dynamic-update-slice.7), channel_id=1, replica_groups=mesh['gx_0'=8,'gx_1'=2,'gy_0'=2,'gy_1'=4,'gz'=2] {'gy_0'}, use_global_device_ids=true, to_apply=%add.12 | all-reduce | flops 4 | bytes 32
  103.5 1.3 dynamic-update-slice.8
  104.8 1.3 dynamic-update-slice.3
  106.8 11.4 %all-reduce.45 = (f32[4]{0:T(128)S(1)}, f32[4]{0:T(128)S(1)}) all-reduce(f32[4]{0:T(128)S(1)} %dynamic-update-slice.3, f32[4]{0:T(128)S(1)} %dynamic-update-slice.8), channel_id=1, replica_groups=mesh['gx_0'=8,'gx_1'=2,'gy_0'=2,'gy_1'=4,'gz'=2] {'gy_1'}, use_global_device_ids=true, to_apply=%add.13 | all-reduce | flops 8 | bytes 64
  122.0 4.9 %all-reduce.48 = (f32[2]{0:T(128)S(1)}, f32[2]{0:T(128)S(1)}) all-reduce(f32[2]{0:T(128)S(1)} %dynamic-update-slice.4, f32[2]{0:T(128)S(1)} %dynamic-update-slice.9), channel_id=1, replica_groups=mesh['gx_0'=8,'gx_1'=2,'gy_0'=2,'gy_1'=4,'gz'=2] {'gz'}, use_global_device_ids=true, to_apply=%add.14 | all-reduce | flops 4 | bytes 32
  129.5 1.3 pad_subtract_fusion
  131.2 1.4 collective-permute-start.16
  132.6 4.6 %collective-permute-start.17 = (f32[1,192,512]{2,1,0:T(8,128)S(1)}, f32[1,192,512]{2,1,0:T(8,128)S(1)}, u32[]{:S(2)}, u32[]{:S(2)}) collective-permute-start(f32[1,192,512]{2,1,0:T(8,128)S(1)} %get-tuple-element.59), channel_id=1, source_target_pairs={{0,1},{2,3},{4,5},{6,7},{8,9},{10,11},{12,13},{14,15},{16,17},{18,... | collective-permute-start | bytes 1179656 | tf_op jit(solution)/shard_map/ppermute | solution.py:39
  137.2 1.5 collective-permute-start.14
  139.7 3.2 %collective-permute-done.12 = f32[2,192,1]{2,1,0:T(8,128)S(1)} collective-permute-done((f32[2,192,1]{2,1,0:T(8,128)S(1)}, f32[2,192,1]{2,1,0:T(8,128)S(1)}, u32[]{:S(2)}, u32[]{:S(2)}) %collective-permute-start.12) | collective-permute-done | bytes 1568 | tf_op jit(solution)/shard_map/ppermute | solution.py:23
  142.8 1.5 collective-permute-start.13
  144.4 4.0 %collective-permute-done.13 = f32[2,192,1]{2,1,0:T(8,128)S(1)} collective-permute-done((f32[2,192,1]{2,1,0:T(8,128)S(1)}, f32[2,192,1]{2,1,0:T(8,128)S(1)}, u32[]{:S(2)}, u32[]{:S(2)}) %collective-permute-start.13) | collective-permute-done | bytes 1568 | tf_op jit(solution)/shard_map/ppermute | solution.py:22
  148.4 3.2 %multiply_reduce_fusion.2 = (f32[]{:T(128)}, f32[]{:T(128)}, f32[2,192,512]{2,1,0:T(8,128)}) fusion(f32[1,192,512]{2,1,0:T(8,128)S(1)} %get-tuple-element.59, f32[1,192,512]{2,1,0:T(8,128)S(1)} %get-tuple-element.58, f32[1,192,512]{2,1,0:T(8,128)S(1)} %collective-permute-done.17, f32[1,192,512]{2,1,0:T(8,128)S(1)} %collective-permute-done.16, ...), kind=kLoop, calls=%fused_computation.133 | loop fusion | flops 9043966 | bytes 8662028 | tf_op jit(solution)/shard_map/reduce_sum | solution.py:103
  151.6 1.3 dynamic-update-slice.15
  152.9 1.4 dynamic-update-slice.10
  154.3 15.6 %all-reduce.41 = (f32[8]{0:T(128)S(1)}, f32[8]{0:T(128)S(1)}) all-reduce(f32[8]{0:T(128)S(1)} %dynamic-update-slice.10, f32[8]{0:T(128)S(1)} %dynamic-update-slice.15), channel_id=1, replica_groups=mesh['gx_0'=8,'gx_1'=2,'gy_0'=2,'gy_1'=4,'gz'=2] {'gx_0'}, use_global_device_ids=true, to_apply=%add.20 | all-reduce | flops 16 | bytes 128
  173.8 2.4 all-reduce.53
  176.9 1.3 dynamic-update-slice.17
  178.9 1.3 dynamic-update-slice.12
  180.2 6.4 %all-reduce.50 = (f32[2]{0:T(128)S(1)}, f32[2]{0:T(128)S(1)}) all-reduce(f32[2]{0:T(128)S(1)} %dynamic-update-slice.12, f32[2]{0:T(128)S(1)} %dynamic-update-slice.17), channel_id=1, replica_groups=mesh['gx_0'=8,'gx_1'=2,'gy_0'=2,'gy_1'=4,'gz'=2] {'gy_0'}, use_global_device_ids=true, to_apply=%add.22 | all-reduce | flops 4 | bytes 32
  187.3 1.3 dynamic-update-slice.18
  190.5 11.4 %all-reduce.44 = (f32[4]{0:T(128)S(1)}, f32[4]{0:T(128)S(1)}) all-reduce(f32[4]{0:T(128)S(1)} %dynamic-update-slice.13, f32[4]{0:T(128)S(1)} %dynamic-update-slice.18), channel_id=1, replica_groups=mesh['gx_0'=8,'gx_1'=2,'gy_0'=2,'gy_1'=4,'gz'=2] {'gy_1'}, use_global_device_ids=true, to_apply=%add.23 | all-reduce | flops 8 | bytes 64
  205.7 4.9 %all-reduce.47 = (f32[2]{0:T(128)S(1)}, f32[2]{0:T(128)S(1)}) all-reduce(f32[2]{0:T(128)S(1)} %dynamic-update-slice.14, f32[2]{0:T(128)S(1)} %dynamic-update-slice.19), channel_id=1, replica_groups=mesh['gx_0'=8,'gx_1'=2,'gy_0'=2,'gy_1'=4,'gz'=2] {'gz'}, use_global_device_ids=true, to_apply=%add.24 | all-reduce | flops 4 | bytes 32
  216.4 1.7 multiply_subtract_fusion.1
  218.3 1.4 collective-permute-start.22
  219.8 4.6 %collective-permute-start.23 = (f32[1,192,512]{2,1,0:T(8,128)S(1)}, f32[1,192,512]{2,1,0:T(8,128)S(1)}, u32[]{:S(2)}, u32[]{:S(2)}) collective-permute-start(f32[1,192,512]{2,1,0:T(8,128)S(1)} %get-tuple-element.56), channel_id=1, source_target_pairs={{0,1},{2,3},{4,5},{6,7},{8,9},{10,11},{12,13},{14,15},{16,17},{18,... | collective-permute-start | bytes 1179656 | tf_op jit(solution)/shard_map/ppermute | solution.py:39
  226.6 3.2 %collective-permute-done.18 = f32[2,192,1]{2,1,0:T(8,128)S(1)} collective-permute-done((f32[2,192,1]{2,1,0:T(8,128)S(1)}, f32[2,192,1]{2,1,0:T(8,128)S(1)}, u32[]{:S(2)}, u32[]{:S(2)}) %collective-permute-start.18) | collective-permute-done | bytes 1568 | tf_op jit(solution)/shard_map/ppermute | solution.py:23
  230.3 5.1 %collective-permute-done.19 = f32[2,192,1]{2,1,0:T(8,128)S(1)} collective-permute-done((f32[2,192,1]{2,1,0:T(8,128)S(1)}, f32[2,192,1]{2,1,0:T(8,128)S(1)}, u32[]{:S(2)}, u32[]{:S(2)}) %collective-permute-start.19) | collective-permute-done | bytes 1568 | tf_op jit(solution)/shard_map/ppermute | solution.py:22
  235.4 3.2 %multiply_reduce_fusion = (f32[]{:T(128)}, f32[]{:T(128)}, f32[2,192,512]{2,1,0:T(8,128)}) fusion(f32[1,192,512]{2,1,0:T(8,128)S(1)} %get-tuple-element.56, f32[1,192,512]{2,1,0:T(8,128)S(1)} %get-tuple-element.55, f32[2,192,512]{2,1,0:T(8,128)S(1)} %multiply_subtract_fusion.1, f32[1,192,512]{2,1,0:T(8,128)S(1)} %collective-permute-done.23, ...), kind=kLoop, calls=%fused_computation.129 | loop fusion | flops 8650750 | bytes 8268808 | tf_op jit(solution)/shard_map/reduce_sum | solution.py:103
  238.6 1.4 dynamic-update-slice.25
  240.0 1.4 dynamic-update-slice.20
  241.4 16.5 %all-reduce.40 = (f32[8]{0:T(128)S(1)}, f32[8]{0:T(128)S(1)}) all-reduce(f32[8]{0:T(128)S(1)} %dynamic-update-slice.20, f32[8]{0:T(128)S(1)} %dynamic-update-slice.25), channel_id=1, replica_groups=mesh['gx_0'=8,'gx_1'=2,'gy_0'=2,'gy_1'=4,'gz'=2] {'gx_0'}, use_global_device_ids=true, to_apply=%add.30 | all-reduce | flops 16 | bytes 128
  258.5 1.3 dynamic-update-slice.26
  260.5 1.3 dynamic-update-slice.21
  261.8 2.4 all-reduce.52
  264.9 1.4 dynamic-update-slice.27
  266.9 1.4 dynamic-update-slice.22
  268.3 6.4 %all-reduce.49 = (f32[2]{0:T(128)S(1)}, f32[2]{0:T(128)S(1)}) all-reduce(f32[2]{0:T(128)S(1)} %dynamic-update-slice.22, f32[2]{0:T(128)S(1)} %dynamic-update-slice.27), channel_id=1, replica_groups=mesh['gx_0'=8,'gx_1'=2,'gy_0'=2,'gy_1'=4,'gz'=2] {'gy_0'}, use_global_device_ids=true, to_apply=%add.32 | all-reduce | flops 4 | bytes 32
  275.3 1.3 dynamic-update-slice.28
  277.3 1.3 dynamic-update-slice.23
  278.6 10.8 %all-reduce.43 = (f32[4]{0:T(128)S(1)}, f32[4]{0:T(128)S(1)}) all-reduce(f32[4]{0:T(128)S(1)} %dynamic-update-slice.23, f32[4]{0:T(128)S(1)} %dynamic-update-slice.28), channel_id=1, replica_groups=mesh['gx_0'=8,'gx_1'=2,'gy_0'=2,'gy_1'=4,'gz'=2] {'gy_1'}, use_global_device_ids=true, to_apply=%add.33 | all-reduce | flops 8 | bytes 64
  293.3 4.9 %all-reduce.46 = (f32[2]{0:T(128)S(1)}, f32[2]{0:T(128)S(1)}) all-reduce(f32[2]{0:T(128)S(1)} %dynamic-update-slice.24, f32[2]{0:T(128)S(1)} %dynamic-update-slice.29), channel_id=1, replica_groups=mesh['gx_0'=8,'gx_1'=2,'gy_0'=2,'gy_1'=4,'gz'=2] {'gz'}, use_global_device_ids=true, to_apply=%add.34 | all-reduce | flops 4 | bytes 32
  303.3 4.4 %multiply_subtract_fusion = (f32[2,192,512]{2,1,0:T(8,128)}, f32[2,192,512]{2,1,0:T(8,128)}) fusion(f32[2,192,512]{2,1,0:T(8,128)} %copy-done.4, f32[2,192,512]{2,1,0:T(8,128)} %get-tuple-element.54, f32[]{:T(128)S(6)} %div.60, f32[]{:T(128)S(6)} %div.62, f32[2,192,512]{2,1,0:T(8,128)} %get-tuple-element.57, f32[2,192,512]{2,1,0:T(8,128)} %get-tuple-element.60, ...), kind=kLoop, calls=%fused_computation.127 | loop fusion | flops 3538944 | bytes 7077908 | tf_op jit(solution)/shard_map/sub | solution.py:166
  (176 shorter events, 53.7 us)
Async XLA Ops:
  1.9 6.1 %copy-start.21 = (f32[2,8]{1,0:T(2,128)S(1)}, f32[2,8]{1,0:T(2,128)}, u32[]{:S(2)}) copy-start(f32[2,8]{1,0:T(2,128)} %param.13) | copy-start | bytes 196
  1.9 6.4 %copy-start.14 = (s32[2,192,512]{2,1,0:T(8,128)S(1)}, s32[2,192,512]{2,1,0:T(8,128)}, u32[]{:S(2)}) copy-start(s32[2,192,512]{2,1,0:T(8,128)} %param.11) | copy-start | bytes 2359300
  4.6 10.9 %collective-permute-start = (f32[2,192,1]{2,1,0:T(8,128)}, f32[2,192,1]{2,1,0:T(8,128)S(1)}, u32[]{:S(2)}, u32[]{:S(2)}) collective-permute-start(f32[2,192,1]{2,1,0:T(8,128)} %get-tuple-element.77), channel_id=1, source_target_pairs={{0,16},{16,32},{32,48},{48,64},{64,80},{80,96},{96,112},{112,128},... | collective-permute-start | bytes 4616 | tf_op jit(solution)/shard_map/ppermute | solution.py:22
  4.6 15.6 %collective-permute-start.1 = (f32[2,192,1]{2,1,0:T(8,128)S(1)}, f32[2,192,1]{2,1,0:T(8,128)S(1)}, u32[]{:S(2)}, u32[]{:S(2)}) collective-permute-start(f32[2,192,1]{2,1,0:T(8,128)S(1)} %get-tuple-element.78), channel_id=1, source_target_pairs={{16,0},{32,16},{48,32},{64,48},{80,64},{96,80},{112,96},{128,112},... | collective-permute-start | bytes 4616 | tf_op jit(solution)/shard_map/ppermute | solution.py:23
  6.3 14.2 %collective-permute-start.2 = (f32[2,1,512]{2,1,0:T(1,128)S(1)}, f32[2,1,512]{2,1,0:T(1,128)S(1)}, u32[]{:S(2)}, u32[]{:S(2)}) collective-permute-start(f32[2,1,512]{2,1,0:T(1,128)S(1)} %get-tuple-element.75), channel_id=1, source_target_pairs={{0,2},{2,4},{4,6},{6,8},{8,10},{10,12},{12,14},{14,0},{1,3},{3,5},... | collective-permute-start | bytes 12296 | tf_op jit(solution)/shard_map/ppermute | solution.py:22
  8.9 6.4 %copy-start.12 = (f32[2,192,512]{2,1,0:T(8,128)}, f32[2,192,512]{2,1,0:T(8,128)S(1)}, u32[]{:S(2)}) copy-start(f32[2,192,512]{2,1,0:T(8,128)S(1)} %select_add_fusion) | copy-start | bytes 2359300
  8.9 6.4 %copy-start.17 = (s32[192,512]{1,0:T(8,128)S(1)}, s32[192,512]{1,0:T(8,128)}, u32[]{:S(2)}) copy-start(s32[192,512]{1,0:T(8,128)} %param.9) | copy-start | bytes 1179652
  9.9 13.6 %collective-permute-start.4 = (f32[1,192,512]{2,1,0:T(8,128)}, f32[1,192,512]{2,1,0:T(8,128)}, u32[]{:S(2)}, u32[]{:S(2)}) collective-permute-start(f32[1,192,512]{2,1,0:T(8,128)} %get-tuple-element.79), channel_id=1, source_target_pairs={{0,1},{2,3},{4,5},{6,7},{8,9},{10,11},{12,13},{14,15},{16,17},{18,... | collective-permute-start | bytes 1179656 | tf_op jit(solution)/shard_map/ppermute | solution.py:39
  14.0 13.0 %collective-permute-start.5 = (f32[1,192,512]{2,1,0:T(8,128)}, f32[1,192,512]{2,1,0:T(8,128)}, u32[]{:S(2)}, u32[]{:S(2)}) collective-permute-start(f32[1,192,512]{2,1,0:T(8,128)} %get-tuple-element.80), channel_id=1, source_target_pairs={{1,0},{3,2},{5,4},{7,6},{9,8},{11,10},{13,12},{15,14},{17,16},{19,... | collective-permute-start | bytes 1179656 | tf_op jit(solution)/shard_map/ppermute | solution.py:42
  15.4 13.0 %copy-start.5 = (f32[1,192,512]{2,1,0:T(8,128)}, f32[1,192,512]{2,1,0:T(8,128)S(1)}, u32[]{:S(2)}) copy-start(f32[1,192,512]{2,1,0:T(8,128)S(1)} %select_bitcast_fusion) | copy-start | bytes 1179652
  15.4 5.1 %copy-start.15 = (f32[2,192,1]{2,1,0:T(8,128)}, f32[2,192,1]{2,1,0:T(8,128)S(1)}, u32[]{:S(2)}) copy-start(f32[2,192,1]{2,1,0:T(8,128)S(1)} %collective-permute-done) | copy-start | bytes 4612
  15.4 6.7 %collective-permute-start.3 = (f32[2,1,512]{2,1,0:T(1,128)S(1)}, f32[2,1,512]{2,1,0:T(1,128)S(1)}, u32[]{:S(2)}, u32[]{:S(2)}) collective-permute-start(f32[2,1,512]{2,1,0:T(1,128)S(1)} %get-tuple-element.76), channel_id=1, source_target_pairs={{2,0},{4,2},{6,4},{8,6},{10,8},{12,10},{14,12},{0,14},{3,1},{5,3},... | collective-permute-start | bytes 12296 | tf_op jit(solution)/shard_map/ppermute | solution.py:23
  20.2 0.7 copy-start.16
  20.5 6.5 %copy-start.13 = (f32[2,192,512]{2,1,0:T(8,128)S(1)}, f32[2,192,512]{2,1,0:T(8,128)}, u32[]{:S(2)}) copy-start(f32[2,192,512]{2,1,0:T(8,128)} %copy-done.12) | copy-start | bytes 2359300
  28.4 1.0 copy-start.18
  28.4 1.1 copy-start.19
  29.5 1.0 copy-start.1
  31.5 21.2 %copy-start.26 = (u32[256]{0:T(256)S(1)}, u32[256]{0:T(256)}, u32[]{:S(2)}) copy-start(u32[256]{0:T(256)} %constant.56) | copy-start | bytes 3076
  31.5 24.7 %collective-permute-start.10 = (f32[1,192,512]{2,1,0:T(8,128)}, f32[1,192,512]{2,1,0:T(8,128)}, u32[]{:S(2)}, u32[]{:S(2)}) collective-permute-start(f32[1,192,512]{2,1,0:T(8,128)} %subtract_bitcast_fusion), channel_id=1, source_target_pairs={{1,0},{3,2},{5,4},{7,6},{9,8},{11,10},{13,12},{15,14},{17,16},{19,... | collective-permute-start | bytes 1179656 | tf_op jit(solution)/shard_map/ppermute | solution.py:42
  32.9 23.3 %collective-permute-start.11 = (f32[1,192,512]{2,1,0:T(8,128)}, f32[1,192,512]{2,1,0:T(8,128)}, u32[]{:S(2)}, u32[]{:S(2)}) collective-permute-start(f32[1,192,512]{2,1,0:T(8,128)} %get-tuple-element.61), channel_id=1, source_target_pairs={{0,1},{2,3},{4,5},{6,7},{8,9},{10,11},{12,13},{14,15},{16,17},{18,... | collective-permute-start | bytes 1179656 | tf_op jit(solution)/shard_map/ppermute | solution.py:39
  39.7 16.5 %collective-permute-start.8 = (f32[2,1,512]{2,1,0:T(1,128)S(1)}, f32[2,1,512]{2,1,0:T(1,128)S(1)}, u32[]{:S(2)}, u32[]{:S(2)}) collective-permute-start(f32[2,1,512]{2,1,0:T(1,128)S(1)} %get-tuple-element.71), channel_id=1, source_target_pairs={{2,0},{4,2},{6,4},{8,6},{10,8},{12,10},{14,12},{0,14},{3,1},{5,3},... | collective-permute-start | bytes 12296 | tf_op jit(solution)/shard_map/ppermute | solution.py:23
  44.6 11.6 %collective-permute-start.9 = (f32[2,1,512]{2,1,0:T(1,128)S(1)}, f32[2,1,512]{2,1,0:T(1,128)S(1)}, u32[]{:S(2)}, u32[]{:S(2)}) collective-permute-start(f32[2,1,512]{2,1,0:T(1,128)S(1)} %get-tuple-element.72), channel_id=1, source_target_pairs={{0,2},{2,4},{4,6},{6,8},{8,10},{10,12},{12,14},{14,0},{1,3},{3,5},... | collective-permute-start | bytes 12296 | tf_op jit(solution)/shard_map/ppermute | solution.py:22
  46.5 3.2 %collective-permute-start.6 = (f32[2,192,1]{2,1,0:T(8,128)S(1)}, f32[2,192,1]{2,1,0:T(8,128)S(1)}, u32[]{:S(2)}, u32[]{:S(2)}) collective-permute-start(f32[2,192,1]{2,1,0:T(8,128)S(1)} %get-tuple-element.74), channel_id=1, source_target_pairs={{16,0},{32,16},{48,32},{64,48},{80,64},{96,80},{112,96},{128,112},... | collective-permute-start | bytes 4616 | tf_op jit(solution)/shard_map/ppermute | solution.py:23
  49.7 0.7 copy-start.20
  50.3 5.9 %collective-permute-start.7 = (f32[2,192,1]{2,1,0:T(8,128)}, f32[2,192,1]{2,1,0:T(8,128)}, u32[]{:S(2)}, u32[]{:S(2)}) collective-permute-start(f32[2,192,1]{2,1,0:T(8,128)} %get-tuple-element.73), channel_id=1, source_target_pairs={{0,16},{16,32},{32,48},{48,64},{64,80},{80,96},{96,112},{112,128},... | collective-permute-start | bytes 4616 | tf_op jit(solution)/shard_map/ppermute | solution.py:22
  56.2 9.1 %copy-start.25 = (u32[256]{0:T(256)S(1)}, u32[256]{0:T(256)}, u32[]{:S(2)}) copy-start(u32[256]{0:T(256)} %constant.61) | copy-start | bytes 3076
  56.2 31.9 %copy-start.24 = (u32[256]{0:T(256)S(1)}, u32[256]{0:T(256)}, u32[]{:S(2)}) copy-start(u32[256]{0:T(256)} %constant.66) | copy-start | bytes 3076
  56.2 38.9 %copy-start.23 = (u32[256]{0:T(256)S(1)}, u32[256]{0:T(256)}, u32[]{:S(2)}) copy-start(u32[256]{0:T(256)} %constant.71) | copy-start | bytes 3076
  56.3 49.9 %copy-start.22 = (u32[256]{0:T(256)S(1)}, u32[256]{0:T(256)}, u32[]{:S(2)}) copy-start(u32[256]{0:T(256)} %constant.76) | copy-start | bytes 3076
  129.5 1.4 copy-start.2
  131.1 20.5 %copy-start.8 = (f32[1,192,512]{2,1,0:T(8,128)}, f32[1,192,512]{2,1,0:T(8,128)S(1)}, u32[]{:S(2)}) copy-start(f32[1,192,512]{2,1,0:T(8,128)S(1)} %get-tuple-element.58) | copy-start | bytes 1179652
  131.1 20.4 %copy-start.9 = (f32[1,192,512]{2,1,0:T(8,128)}, f32[1,192,512]{2,1,0:T(8,128)S(1)}, u32[]{:S(2)}) copy-start(f32[1,192,512]{2,1,0:T(8,128)S(1)} %get-tuple-element.59) | copy-start | bytes 1179652
  131.2 17.3 %copy-start = (f32[2,192,512]{2,1,0:T(8,128)S(1)}, f32[2,192,512]{2,1,0:T(8,128)}, u32[]{:S(2)}) copy-start(f32[2,192,512]{2,1,0:T(8,128)} %get-tuple-element.60) | copy-start | bytes 2359300
  131.2 17.3 %copy-start.6 = (f32[1,192,512]{2,1,0:T(8,128)S(1)}, f32[1,192,512]{2,1,0:T(8,128)}, u32[]{:S(2)}) copy-start(f32[1,192,512]{2,1,0:T(8,128)} %copy-done.5) | copy-start | bytes 1179652
  131.2 17.2 %collective-permute-start.16 = (f32[1,192,512]{2,1,0:T(8,128)S(1)}, f32[1,192,512]{2,1,0:T(8,128)S(1)}, u32[]{:S(2)}, u32[]{:S(2)}) collective-permute-start(f32[1,192,512]{2,1,0:T(8,128)S(1)} %get-tuple-element.58), channel_id=1, source_target_pairs={{1,0},{3,2},{5,4},{7,6},{9,8},{11,10},{13,12},{15,14},{17,16},{19,... | collective-permute-start | bytes 1179656 | tf_op jit(solution)/shard_map/ppermute | solution.py:42
  132.6 15.8 %collective-permute-start.17 = (f32[1,192,512]{2,1,0:T(8,128)S(1)}, f32[1,192,512]{2,1,0:T(8,128)S(1)}, u32[]{:S(2)}, u32[]{:S(2)}) collective-permute-start(f32[1,192,512]{2,1,0:T(8,128)S(1)} %get-tuple-element.59), channel_id=1, source_target_pairs={{0,1},{2,3},{4,5},{6,7},{8,9},{10,11},{12,13},{14,15},{16,17},{18,... | collective-permute-start | bytes 1179656 | tf_op jit(solution)/shard_map/ppermute | solution.py:39
  137.2 11.2 %collective-permute-start.14 = (f32[2,1,512]{2,1,0:T(1,128)S(1)}, f32[2,1,512]{2,1,0:T(1,128)S(1)}, u32[]{:S(2)}, u32[]{:S(2)}) collective-permute-start(f32[2,1,512]{2,1,0:T(1,128)S(1)} %get-tuple-element.67), channel_id=1, source_target_pairs={{2,0},{4,2},{6,4},{8,6},{10,8},{12,10},{14,12},{0,14},{3,1},{5,3},... | collective-permute-start | bytes 12296 | tf_op jit(solution)/shard_map/ppermute | solution.py:23
  138.7 9.7 %collective-permute-start.15 = (f32[2,1,512]{2,1,0:T(1,128)S(1)}, f32[2,1,512]{2,1,0:T(1,128)S(1)}, u32[]{:S(2)}, u32[]{:S(2)}) collective-permute-start(f32[2,1,512]{2,1,0:T(1,128)S(1)} %get-tuple-element.68), channel_id=1, source_target_pairs={{0,2},{2,4},{4,6},{6,8},{8,10},{10,12},{12,14},{14,0},{1,3},{3,5},... | collective-permute-start | bytes 12296 | tf_op jit(solution)/shard_map/ppermute | solution.py:22
  139.6 3.2 %collective-permute-start.12 = (f32[2,192,1]{2,1,0:T(8,128)S(1)}, f32[2,192,1]{2,1,0:T(8,128)S(1)}, u32[]{:S(2)}, u32[]{:S(2)}) collective-permute-start(f32[2,192,1]{2,1,0:T(8,128)S(1)} %get-tuple-element.70), channel_id=1, source_target_pairs={{16,0},{32,16},{48,32},{64,48},{80,64},{96,80},{112,96},{128,112},... | collective-permute-start | bytes 4616 | tf_op jit(solution)/shard_map/ppermute | solution.py:23
  142.8 5.6 %collective-permute-start.13 = (f32[2,192,1]{2,1,0:T(8,128)S(1)}, f32[2,192,1]{2,1,0:T(8,128)S(1)}, u32[]{:S(2)}, u32[]{:S(2)}) collective-permute-start(f32[2,192,1]{2,1,0:T(8,128)S(1)} %get-tuple-element.69), channel_id=1, source_target_pairs={{0,16},{16,32},{32,48},{48,64},{64,80},{80,96},{96,112},{112,128},... | collective-permute-start | bytes 4616 | tf_op jit(solution)/shard_map/ppermute | solution.py:22
  216.4 1.7 copy-start.3
  218.0 17.4 %copy-start.4 = (f32[2,192,512]{2,1,0:T(8,128)}, f32[2,192,512]{2,1,0:T(8,128)S(1)}, u32[]{:S(2)}) copy-start(f32[2,192,512]{2,1,0:T(8,128)S(1)} %multiply_subtract_fusion.1) | copy-start | bytes 2359300
  218.3 20.3 %copy-start.10 = (f32[1,192,512]{2,1,0:T(8,128)}, f32[1,192,512]{2,1,0:T(8,128)S(1)}, u32[]{:S(2)}) copy-start(f32[1,192,512]{2,1,0:T(8,128)S(1)} %get-tuple-element.55) | copy-start | bytes 1179652
  218.3 20.3 %copy-start.11 = (f32[1,192,512]{2,1,0:T(8,128)}, f32[1,192,512]{2,1,0:T(8,128)S(1)}, u32[]{:S(2)}) copy-start(f32[1,192,512]{2,1,0:T(8,128)S(1)} %get-tuple-element.56) | copy-start | bytes 1179652
  218.3 17.1 %copy-start.7 = (f32[1,192,512]{2,1,0:T(8,128)S(1)}, f32[1,192,512]{2,1,0:T(8,128)}, u32[]{:S(2)}) copy-start(f32[1,192,512]{2,1,0:T(8,128)} %copy-done.5) | copy-start | bytes 1179652
  218.3 17.0 %collective-permute-start.22 = (f32[1,192,512]{2,1,0:T(8,128)S(1)}, f32[1,192,512]{2,1,0:T(8,128)S(1)}, u32[]{:S(2)}, u32[]{:S(2)}) collective-permute-start(f32[1,192,512]{2,1,0:T(8,128)S(1)} %get-tuple-element.55), channel_id=1, source_target_pairs={{1,0},{3,2},{5,4},{7,6},{9,8},{11,10},{13,12},{15,14},{17,16},{19,... | collective-permute-start | bytes 1179656 | tf_op jit(solution)/shard_map/ppermute | solution.py:42
  219.8 15.6 %collective-permute-start.23 = (f32[1,192,512]{2,1,0:T(8,128)S(1)}, f32[1,192,512]{2,1,0:T(8,128)S(1)}, u32[]{:S(2)}, u32[]{:S(2)}) collective-permute-start(f32[1,192,512]{2,1,0:T(8,128)S(1)} %get-tuple-element.56), channel_id=1, source_target_pairs={{0,1},{2,3},{4,5},{6,7},{8,9},{10,11},{12,13},{14,15},{16,17},{18,... | collective-permute-start | bytes 1179656 | tf_op jit(solution)/shard_map/ppermute | solution.py:39
  224.4 11.0 %collective-permute-start.20 = (f32[2,1,512]{2,1,0:T(1,128)S(1)}, f32[2,1,512]{2,1,0:T(1,128)S(1)}, u32[]{:S(2)}, u32[]{:S(2)}) collective-permute-start(f32[2,1,512]{2,1,0:T(1,128)S(1)} %get-tuple-element.63), channel_id=1, source_target_pairs={{2,0},{4,2},{6,4},{8,6},{10,8},{12,10},{14,12},{0,14},{3,1},{5,3},... | collective-permute-start | bytes 12296 | tf_op jit(solution)/shard_map/ppermute | solution.py:23
  225.6 9.8 %collective-permute-start.21 = (f32[2,1,512]{2,1,0:T(1,128)S(1)}, f32[2,1,512]{2,1,0:T(1,128)S(1)}, u32[]{:S(2)}, u32[]{:S(2)}) collective-permute-start(f32[2,1,512]{2,1,0:T(1,128)S(1)} %get-tuple-element.64), channel_id=1, source_target_pairs={{0,2},{2,4},{4,6},{6,8},{8,10},{10,12},{12,14},{14,0},{1,3},{3,5},... | collective-permute-start | bytes 12296 | tf_op jit(solution)/shard_map/ppermute | solution.py:22
  226.6 3.2 %collective-permute-start.18 = (f32[2,192,1]{2,1,0:T(8,128)S(1)}, f32[2,192,1]{2,1,0:T(8,128)S(1)}, u32[]{:S(2)}, u32[]{:S(2)}) collective-permute-start(f32[2,192,1]{2,1,0:T(8,128)S(1)} %get-tuple-element.66), channel_id=1, source_target_pairs={{16,0},{32,16},{48,32},{64,48},{80,64},{96,80},{112,96},{128,112},... | collective-permute-start | bytes 4616 | tf_op jit(solution)/shard_map/ppermute | solution.py:23
  229.8 5.6 %collective-permute-start.19 = (f32[2,192,1]{2,1,0:T(8,128)S(1)}, f32[2,192,1]{2,1,0:T(8,128)S(1)}, u32[]{:S(2)}, u32[]{:S(2)}) collective-permute-start(f32[2,192,1]{2,1,0:T(8,128)S(1)} %get-tuple-element.65), channel_id=1, source_target_pairs={{0,16},{16,32},{32,48},{48,64},{64,80},{80,96},{96,112},{112,128},... | collective-permute-start | bytes 4616 | tf_op jit(solution)/shard_map/ppermute | solution.py:22
